TPU v7x, 32 devices: a whole 2x2x4 slice. The times are simulated.
32 devices in a mesh: grp: 2 (over y), mode: 8 (over z, x), node: 2 (over core).
Axes of the slice: x: 2, y: 2, z: 4, core: 2. Of those that a mesh axis runs over, the one named last changes fastest.
Arguments:
- mode_basis: float32 [4096, 4096], P('mode', 'node'), may hold values from -6 to 6
- mode_scales: float32 [4096], P('mode'), may hold values from 0.003 to 0.02
- mean_log: float32 [4096], P(('node', 'mode')), may hold values from -0.5 to 0.5
- sample_seeds: int32 [4096], P('grp'), parts along dimension 0, may hold values from 0 to 1073741823
Outputs:
- modulus: float32 [4096, 4096], P(('node', 'mode'), 'grp'), parts along dimension 1
- sample_means: float32 [4096], P('grp'), parts along dimension 0
There are 2 independent parts, one for each index of `grp`. A program takes and returns all parts, laid end to end along the dimension named above; an argument that names none is the same for every part. Nothing has to cross between parts.
All inputs are finite; a program needn't handle non-finite values.
Results may differ from a plain program's by a relative error of at most 0.00005.
Values sent between devices are 32-bit elements; how exact they have to be, the bound alone decides.
A program may use at most 64 MiB of HBM per device.

v0:
```python
import functools
import math

import jax
import jax.numpy as jnp
import numpy as np
from jax import lax
from jax.experimental import pallas as pl
from jax.experimental.pallas import tpu as pltpu
from jax.sharding import PartitionSpec as P

MESH = pl.DeviceIdType.MESH


def sine_series():
    points = 0.25 * np.cos((np.arange(200) + 0.5) * np.pi / 400)
    powers = points[:, None] ** np.arange(0, 11, 2)[None, :]
    values = np.sin(2 * np.pi * points) / points
    return [float(c) for c in np.linalg.lstsq(powers, values, rcond=None)[0]]


SINE = sine_series()


def scramble(word):
    word = word ^ lax.shift_right_logical(word, jnp.int32(15))
    word = word * jnp.int32(-2048144789)
    word = word ^ lax.shift_right_logical(word, jnp.int32(13))
    word = word * jnp.int32(-1028477387)
    return word ^ lax.shift_right_logical(word, jnp.int32(16))


def normals(seed_terms, counter_terms):
    start_word = seed_terms + counter_terms
    first_word = scramble(start_word) & jnp.int32(16777215)
    second_word = scramble(start_word + jnp.int32(668265261)) & jnp.int32(16777215)
    first_unit = (first_word.astype(jnp.float32) + 0.5) * (1.0 / 16777216.0)
    square = -2.0 * jnp.log(first_unit)
    radius = square * lax.rsqrt(jnp.maximum(square, 1e-30))
    folded = jnp.abs(second_word.astype(jnp.float32) - 8388607.5) - 4194304.0
    turn = folded * (1.0 / 16777216.0)
    turn2 = turn * turn
    series = jnp.full_like(turn, SINE[-1])
    for coefficient in SINE[-2::-1]:
        series = series * turn2 + coefficient
    return (radius * turn) * series


def split(values):
    high = values.astype(jnp.bfloat16)
    return high, (values - high.astype(jnp.float32)).astype(jnp.bfloat16)


def kernel(n, basis, scales, mean, seeds, modulus, means, gathered, scale_all, mean_all, coefs, lhs,
           total, staged, parts, halves, net_send, net_recv, row_send, row_recv, core_send, core_recv,
           scale_send, scale_recv, part_send, part_recv, mean_sems, own_sem, out_sems, half_sems):
    g, me, c = lax.axis_index("grp"), lax.axis_index("mode"), lax.axis_index("node")
    _, _, pieces, piece, wide = gathered.shape
    rows = pieces * piece
    mine, theirs = [[side * 2 + p for p in range(2)] for side in (g, 1 - g)]
    samples = coefs.shape[-1]
    across, sibling = (1 - g, me, c), (g, me, 1 - c)

    def to(step):
        flipped, bit = 0, 1
        while bit < n:
            flipped = flipped + lax.rem(me // bit + step // bit, 2) * bit
            bit *= 2
        return flipped

    near, quarter = n // 2, n // 4

    def far(q):
        return near + lax.rem(q, 2) * quarter + q // 2

    barrier = pltpu.get_barrier_semaphore()

    @pl.loop(1, n)
    def _(step):
        pl.semaphore_signal(barrier, inc=1, device_id=(g, to(step), c), device_id_type=MESH)

    pl.semaphore_signal(barrier, inc=1, device_id=across, device_id_type=MESH)
    pl.semaphore_signal(barrier, inc=1, device_id=sibling, device_id_type=MESH)

    own_scale = scale_all.at[me]
    own_mean = mean_all.at[c]
    own_scale[...] = scales[...]
    own_mean[...] = mean[...]
    own_columns = pl.ds(pl.multiple_of(me * wide, 128), wide)
    own = [
        pltpu.make_async_copy(basis.at[pl.ds(k * piece, piece), own_columns], gathered.at[c, me, k], own_sem.at[k])
        for k in range(pieces)
    ]
    for copy in own:
        copy.start()
    pl.semaphore_wait(barrier, n + 1)

    def net(step, owner, k):
        peer = to(step)
        return pltpu.make_async_remote_copy(
            src_ref=basis.at[pl.ds(pl.multiple_of(k * piece, 8), piece), pl.ds(pl.multiple_of(peer * wide, 128), wide)],
            dst_ref=gathered.at[c, owner, k],
            send_sem=net_send.at[k, step], recv_sem=net_recv.at[k, step], device_id=(g, peer, c), device_id_type=MESH)

    def scale_copy(step, owner):
        return pltpu.make_async_remote_copy(
            src_ref=scales, dst_ref=scale_all.at[owner],
            send_sem=scale_send.at[step], recv_sem=scale_recv.at[step], device_id=(g, to(step), c), device_id_type=MESH)

    def row_copy(step, owner, k, p):
        block = gathered.at[c, owner, k]
        return pltpu.make_async_remote_copy(
            src_ref=block, dst_ref=block,
            send_sem=row_send.at[p, step], recv_sem=row_recv.at[p, step], device_id=across, device_id_type=MESH)

    def core_copy(step, owner, k, side):
        block = gathered.at[side, owner, k]
        return pltpu.make_async_remote_copy(
            src_ref=block, dst_ref=block,
            send_sem=core_send.at[k, step], recv_sem=core_recv.at[k, step],
            device_id=sibling, device_id_type=MESH)

    def part_copy(step, owner):
        return pltpu.make_async_remote_copy(
            src_ref=parts.at[me], dst_ref=parts.at[owner],
            send_sem=part_send.at[step], recv_sem=part_recv.at[step], device_id=(g, to(step), c), device_id_type=MESH)

    mean_copy = lambda side: pltpu.make_async_remote_copy(
        src_ref=mean, dst_ref=mean_all.at[side], send_sem=mean_sems.at[0], recv_sem=mean_sems.at[1],
        device_id=sibling, device_id_type=MESH)

    @pl.loop(1, n)
    def _(step):
        scale_copy(step, me).start()

    mean_copy(c).start()

    @pl.loop(1, quarter)
    def _(step):
        for k in range(pieces):
            net(step, me, k).start()

    @pl.loop(quarter, near)
    def _(step):
        for k in mine:
            net(step, me, k).start()

    @pl.loop(0, near)
    def _(q):
        for k in mine:
            net(far(q), me, k).start()

    for copy in own:
        copy.wait()
    for k in range(pieces):
        core_copy(0, me, k, c).start()

    seed_terms = seeds[:, pl.ds(pl.multiple_of(c * samples, 128), samples)] * jnp.int32(-1640531527)
    lanes = min(512, samples)

    def draw(owner):
        @pl.loop(0, rows // 16)
        def _(tile):
            first = owner * rows + tile * 16
            ids = lax.broadcasted_iota(jnp.int32, (16, lanes), 0) + first
            counters = ids * jnp.int32(2 * 668265261 - 2**32 if 2 * 668265261 >= 2**31 else 2 * 668265261)
            for start in range(0, samples, lanes):
                high, low = split(normals(seed_terms[:, start:start + lanes], counters))
                for part, values in enumerate((high, low, high)):
                    here = pl.ds(pl.multiple_of(part * rows + tile * 16, 16), 16)
                    coefs[owner, here, start:start + lanes] = values

    def multiply(step, owner, first):
        for k in range(pieces):
            core_copy(step, owner, k, 1 - c).wait_recv()
        scale_row = scale_all[owner]
        for side in range(2):
            block = gathered[side, owner].reshape(rows, wide)
            high, low = split(block.T * scale_row)
            for part, values in enumerate((high, high, low)):
                lhs[side * wide:(side + 1) * wide, part * rows:(part + 1) * rows] = values
        columns = min(1024, samples)

        @pl.loop(0, samples // columns)
        def _(tile):
            here = pl.ds(pl.multiple_of(tile * columns, 128), columns)
            product = jnp.dot(lhs[...], coefs[owner, :, here], preferred_element_type=jnp.float32)
            if first:
                total[:, here] = product
            else:
                total[:, here] += product

    draw(me)

    def forward(step):
        owner = to(step)
        for p, k in enumerate(mine):
            net(step, owner, k).wait_recv()
            row_copy(step, owner, k, p).start()
            core_copy(step, owner, k, c).start()

    def finish(step):
        owner = to(step)
        for p, k in enumerate(theirs):
            row_copy(step, owner, k, p).wait_recv()
            core_copy(step, owner, k, c).start()

    def use(step):
        scale_copy(step, to(step)).wait_recv()
        multiply(step, to(step), False)

    @pl.loop(1, quarter)
    def _(step):
        draw(to(step))

    multiply(0, me, True)

    @pl.loop(0, quarter)
    def _(q):
        draw(to(quarter + q))
        forward(quarter + q)
        draw(to(far(q)))
        draw(to(far(quarter + q)))
        forward(far(q))

    @pl.loop(1, quarter)
    def _(step):
        for k in range(pieces):
            net(step, to(step), k).wait_recv()
            core_copy(step, to(step), k, c).start()

    @pl.loop(quarter, near)
    def _(step):
        finish(step)

    @pl.loop(1, near - quarter // 2)
    def _(step):
        use(step)

    @pl.loop(quarter, near)
    def _(q):
        forward(far(q))

    @pl.loop(0, quarter)
    def _(q):
        finish(far(q))

    @pl.loop(near - quarter // 2, near)
    def _(step):
        use(step)

    @pl.loop(0, quarter)
    def _(q):
        use(far(q))
        finish(far(quarter + q))

    @pl.loop(quarter, near)
    def _(q):
        use(far(q))

    mean_copy(1 - c).wait_recv()

    sums = jnp.zeros((1, samples), jnp.float32)
    for side in range(2):
        shift = jnp.broadcast_to(mean_all[side], (8, wide)).T[:, :1]
        values = jnp.exp(total[side * wide:(side + 1) * wide, :] + shift)
        staged[side] = values
        sums = sums + jnp.sum(values, axis=0, keepdims=True)
    parts[me] = sums
    out_columns = modulus.at[:, pl.ds(pl.multiple_of(c * samples, 128), samples)]
    other_columns = modulus.at[:, pl.ds(pl.multiple_of((1 - c) * samples, 128), samples)]
    local_out = pltpu.make_async_copy(staged.at[c], out_columns, out_sems.at[0])
    send_out = lambda landing: pltpu.make_async_remote_copy(
        src_ref=staged.at[1 - c], dst_ref=landing, send_sem=out_sems.at[1], recv_sem=out_sems.at[2],
        device_id=sibling, device_id_type=MESH)

    @pl.loop(1, n)
    def _(step):
        part_copy(step, me).start()

    send_out(out_columns).start()
    local_out.start()

    @pl.loop(1, n)
    def _(step):
        part_copy(step, to(step)).wait_recv()

    summed = jnp.zeros((1, samples), jnp.float32)
    for m in range(n):
        summed = summed + parts[m]
    halves[c] = summed / (n * 2 * wide)
    half_copy = lambda side: pltpu.make_async_remote_copy(
        src_ref=halves.at[c], dst_ref=halves.at[side], send_sem=half_sems.at[0], recv_sem=half_sems.at[1],
        device_id=sibling, device_id_type=MESH)
    half_copy(c).start()

    mean_copy(c).wait_send()
    for k in range(pieces):
        core_copy(0, me, k, c).wait_send()

    @pl.loop(1, n)
    def _(step):
        scale_copy(step, me).wait_send()
        part_copy(step, me).wait_send()
        for k in range(pieces):
            core_copy(step, to(step), k, c).wait_send()
        for k in mine:
            net(step, me, k).wait_send()

    @pl.loop(1, quarter)
    def _(step):
        for k in theirs:
            net(step, me, k).wait_send()

    @pl.loop(quarter, n)
    def _(step):
        for p, k in enumerate(mine):
            row_copy(step, to(step), k, p).wait_send()

    half_copy(1 - c).wait_recv()
    half_copy(c).wait_send()
    means[:, 0:samples] = halves[0]
    means[:, samples:2 * samples] = halves[1]
    local_out.wait()
    send_out(other_columns).wait_recv()
    send_out(out_columns).wait_send()


def on_device(mode_basis, mode_scales, mean_log, sample_seeds):
    n = lax.axis_size("mode")
    rows, wide, all_samples = mode_scales.shape[0], mean_log.shape[0], sample_seeds.shape[0]
    piece, samples = rows // 4, all_samples // 2
    vmem = pl.BlockSpec(memory_space=pltpu.VMEM)
    anywhere = pl.BlockSpec(memory_space=pl.ANY)
    dma = pltpu.SemaphoreType.DMA
    modulus, means = pl.pallas_call(
        functools.partial(kernel, n),
        out_shape=(
            jax.ShapeDtypeStruct((wide, all_samples), jnp.float32),
            jax.ShapeDtypeStruct((1, all_samples), jnp.float32),
        ),
        in_specs=[anywhere, vmem, vmem, vmem],
        out_specs=(anywhere, vmem),
        scratch_shapes=[
            pltpu.VMEM((2, n, 4, piece, wide), jnp.float32),
            pltpu.VMEM((n, 1, rows), jnp.float32),
            pltpu.VMEM((2, 1, wide), jnp.float32),
            pltpu.VMEM((n, 3 * rows, samples), jnp.bfloat16),
            pltpu.VMEM((2 * wide, 3 * rows), jnp.bfloat16),
            pltpu.VMEM((2 * wide, samples), jnp.float32),
            pltpu.VMEM((2, wide, samples), jnp.float32),
            pltpu.VMEM((n, 1, samples), jnp.float32),
            pltpu.VMEM((2, 1, samples), jnp.float32),
            dma((4, n)), dma((4, n)), dma((2, n)), dma((2, n)), dma((4, n)), dma((4, n)),
            dma((n,)), dma((n,)), dma((n,)), dma((n,)), dma((2,)), dma((4,)), dma((3,)), dma((2,)),
        ],
        compiler_params=pltpu.CompilerParams(
            collective_id=0, has_side_effects=True, vmem_limit_bytes=60 * 1024 * 1024
        ),
    )(mode_basis, mode_scales[None, :], mean_log[None, :], sample_seeds[None, :])
    return modulus, means[0]


def solution(mesh):
    return jax.shard_map(
        on_device,
        mesh=mesh,
        in_specs=(P("mode", "node"), P("mode"), P(("node", "mode")), P("grp")),
        out_specs=(P(("node", "mode"), "grp"), P("grp")),
        check_vma=False,
    )
```

profile of v0, /device:TPU:0, one launch (start us, length us, event | category | flops | bytes accessed | tf_op | source)
XLA Modules:
  0.0 76.0 jit_solution(11960361197375803839)
XLA Ops:
  0.6 71.6 %shard_map.59 = (f32[256,2048]{1,0:T(8,128)}, f32[1,2048]{1,0:T(1,128)}) custom-call(f32[512,2048]{1,0:T(8,128)} %basis.1, f32[1,512]{1,0:T(1,128)} %bitcast.6, f32[1,256]{1,0:T(1,128)} %bitcast.7, s32[1,2048]{1,0:T(1,128)} %bitcast.4), custom_call_target="tpu_custom_call" | custom-call | tf_op jit(solution)/shard_map/pallas_call | solution.py:336
  72.2 0.0 copy-start
  72.2 3.1 %copy.8 = f32[256,2048]{1,0:T(8,128)} copy(f32[256,2048]{1,0:T(8,128)} %get-tuple-element.8) | data formatting | bytes 4194304
  75.4 0.0 copy-done
  75.4 0.6 copy.9
Async XLA Ops:
  72.2 3.2 %copy-start = (f32[1,2048]{1,0:T(1,128)S(1)}, f32[1,2048]{1,0:T(1,128)}, u32[]{:S(2)}) copy-start(f32[1,2048]{1,0:T(1,128)} %get-tuple-element.5) | copy-start | bytes 24580
where the time goes:
time: 76.2 us; the launch traced here: 76 us
  Pallas kernels  71.6 us (94%)
  local copies, waits for them, and re-layouts  3.74 us (5%)
    pallas_call x1, Pallas kernels, on_device(): pl.pallas_call(functools.partial(kernel, n), out_shape=(jax.ShapeDtypeStr...  71.6 us
    unnamed x4, local copies, waits for them, and re-layouts  3.74 us

commit v1 on v0

--- a/solution.py
+++ b/solution.py
@@ -68,10 +68,21 @@
             bit *= 2
         return flipped
 
-    near, quarter = n // 2, n // 4
+    near, quarter, eighth = n // 2, n // 4, n // 8
+    inner = lax.rem(me // near + me // quarter, 2)
 
     def far(q):
-        return near + lax.rem(q, 2) * quarter + q // 2
+        return near + quarter - 1 - q // 2 + lax.rem(q, 2) * quarter
+
+    def relay(j):
+        base = n - 1 - j
+        return base + inner * (quarter * (1 - 2 * ((base // quarter) % 2)))
+
+    def each(low, high, body):
+        if high - low == 1:
+            body(low)
+        else:
+            pl.loop(low, high)(body)
 
     barrier = pltpu.get_barrier_semaphore()
 
@@ -135,21 +146,21 @@
 
     mean_copy(c).start()
 
-    @pl.loop(1, quarter)
-    def _(step):
-        for k in range(pieces):
-            net(step, me, k).start()
-
-    @pl.loop(quarter, near)
-    def _(step):
-        for k in mine:
-            net(step, me, k).start()
-
     @pl.loop(0, near)
     def _(q):
         for k in mine:
             net(far(q), me, k).start()
 
+    @pl.loop(quarter, near)
+    def _(step):
+        for k in range(pieces):
+            net(step, me, k).start()
+
+    @pl.loop(1, quarter)
+    def _(step):
+        for k in range(pieces):
+            net(step, me, k).start()
+
     for copy in own:
         copy.wait()
     for k in range(pieces):
@@ -158,105 +169,132 @@
     seed_terms = seeds[:, pl.ds(pl.multiple_of(c * samples, 128), samples)] * jnp.int32(-1640531527)
     lanes = min(512, samples)
 
-    def draw(owner):
-        @pl.loop(0, rows // 16)
+    half = rows // 2
+    tiles = half // 16
+
+    def draw_half(owner, side):
+        @pl.loop(0, tiles)
         def _(tile):
-            first = owner * rows + tile * 16
+            first = owner * rows + side * half + tile * 16
             ids = lax.broadcasted_iota(jnp.int32, (16, lanes), 0) + first
             counters = ids * jnp.int32(2 * 668265261 - 2**32 if 2 * 668265261 >= 2**31 else 2 * 668265261)
             for start in range(0, samples, lanes):
                 high, low = split(normals(seed_terms[:, start:start + lanes], counters))
                 for part, values in enumerate((high, low, high)):
-                    here = pl.ds(pl.multiple_of(part * rows + tile * 16, 16), 16)
+                    here = pl.ds(pl.multiple_of((3 * side + part) * half + tile * 16, 16), 16)
                     coefs[owner, here, start:start + lanes] = values
 
-    def multiply(step, owner, first):
-        for k in range(pieces):
-            core_copy(step, owner, k, 1 - c).wait_recv()
-        scale_row = scale_all[owner]
-        for side in range(2):
-            block = gathered[side, owner].reshape(rows, wide)
-            high, low = split(block.T * scale_row)
-            for part, values in enumerate((high, high, low)):
-                lhs[side * wide:(side + 1) * wide, part * rows:(part + 1) * rows] = values
+    def draw(owner):
+        draw_half(owner, 0)
+        draw_half(owner, 1)
+
+    def accumulate(owner, first_row, depth, first):
         columns = min(1024, samples)
 
         @pl.loop(0, samples // columns)
         def _(tile):
             here = pl.ds(pl.multiple_of(tile * columns, 128), columns)
-            product = jnp.dot(lhs[...], coefs[owner, :, here], preferred_element_type=jnp.float32)
+            product = jnp.dot(lhs[:, 0:depth], coefs[owner, pl.ds(first_row, depth), here], preferred_element_type=jnp.float32)
             if first:
                 total[:, here] = product
             else:
                 total[:, here] += product
 
-    draw(me)
-
-    def forward(step):
+    def multiply(step, owner, first):
+        for k in range(pieces):
+            core_copy(step, owner, k, 1 - c).wait_recv()
+        for side in range(2):
+            block = gathered[side, owner].reshape(rows, wide)
+            high, low = split(block.T * scale_all[owner])
+            for h in range(2):
+                for part, values in enumerate((high, high, low)):
+                    at = (3 * h + part) * half
+                    lhs[side * wide:(side + 1) * wide, at:at + half] = values[:, h * half:(h + 1) * half]
+        accumulate(owner, 0, 3 * rows, first)
+
+    def multiply_half(step, h, ks):
         owner = to(step)
-        for p, k in enumerate(mine):
-            net(step, owner, k).wait_recv()
-            row_copy(step, owner, k, p).start()
-            core_copy(step, owner, k, c).start()
-
-    def finish(step):
-        owner = to(step)
-        for p, k in enumerate(theirs):
-            row_copy(step, owner, k, p).wait_recv()
-            core_copy(step, owner, k, c).start()
+        for k in ks:
+            core_copy(step, owner, k, 1 - c).wait_recv()
+        scale_row = jnp.where(h == 0, scale_all[owner][:, 0:half], scale_all[owner][:, half:rows])
+        for side in range(2):
+            block = gathered[side, owner, pl.ds(h * (pieces // 2), pieces // 2)].reshape(half, wide)
+            high, low = split(block.T * scale_row)
+            for part, values in enumerate((high, high, low)):
+                lhs[side * wide:(side + 1) * wide, part * half:(part + 1) * half] = values
+        accumulate(owner, pl.multiple_of(h * (3 * half), 16), 3 * half, False)
+
+    def forward(j, p):
+        step = relay(j)
+        owner, k = to(step), mine[p]
+        net(step, owner, k).wait_recv()
+        row_copy(step, owner, k, p).start()
+        core_copy(step, owner, k, c).start()
+
+    def finish(j, p):
+        step = relay(j)
+        owner, k = to(step), theirs[p]
+        row_copy(step, owner, k, p).wait_recv()
+        core_copy(step, owner, k, c).start()
+
+    def share(step):
+        for k in range(pieces):
+            net(step, to(step), k).wait_recv()
+            core_copy(step, to(step), k, c).start()
 
     def use(step):
         scale_copy(step, to(step)).wait_recv()
         multiply(step, to(step), False)
 
-    @pl.loop(1, quarter)
-    def _(step):
-        draw(to(step))
-
+    def group(index):
+        return index * eighth, (index + 1) * eighth
+
+    draw(me)
+    each(1, quarter, lambda step: draw(to(step)))
     multiply(0, me, True)
-
-    @pl.loop(0, quarter)
-    def _(q):
-        draw(to(quarter + q))
-        forward(quarter + q)
-        draw(to(far(q)))
-        draw(to(far(quarter + q)))
-        forward(far(q))
-
-    @pl.loop(1, quarter)
-    def _(step):
-        for k in range(pieces):
-            net(step, to(step), k).wait_recv()
-            core_copy(step, to(step), k, c).start()
-
-    @pl.loop(quarter, near)
-    def _(step):
-        finish(step)
-
-    @pl.loop(1, near - quarter // 2)
-    def _(step):
-        use(step)
-
-    @pl.loop(quarter, near)
-    def _(q):
-        forward(far(q))
-
-    @pl.loop(0, quarter)
-    def _(q):
-        finish(far(q))
-
-    @pl.loop(near - quarter // 2, near)
-    def _(step):
-        use(step)
-
-    @pl.loop(0, quarter)
-    def _(q):
-        use(far(q))
-        finish(far(quarter + q))
-
-    @pl.loop(quarter, near)
-    def _(q):
-        use(far(q))
+    each(*group(0), lambda j: draw(to(relay(j))))
+    each(*group(0), lambda j: forward(j, 0))
+    each(*group(1), lambda j: draw_half(to(relay(j)), 0))
+    each(*group(0), lambda j: forward(j, 1))
+    each(*group(1), lambda j: draw_half(to(relay(j)), 1))
+    each(*group(2), lambda step: draw_half(to(step), 0))
+    each(*group(0), lambda j: finish(j, 0))
+    each(*group(2), lambda step: draw_half(to(step), 1))
+    each(*group(0), lambda j: finish(j, 1))
+    each(1, quarter, share)
+    each(1, quarter, use)
+    each(*group(0), lambda j: use(relay(j)))
+    each(*group(1), lambda j: forward(j, 0))
+    each(*group(2), lambda j: draw_half(to(relay(j)), 0))
+    each(*group(1), lambda j: forward(j, 1))
+    each(*group(2), lambda j: draw_half(to(relay(j)), 1))
+    each(*group(1), lambda j: finish(j, 0))
+    each(*group(3), lambda step: draw_half(to(step), 0))
+    each(*group(1), lambda j: finish(j, 1))
+    each(*group(3), lambda step: draw_half(to(step), 1))
+    each(*group(1), lambda j: use(relay(j)))
+    each(*group(2), lambda j: forward(j, 0))
+    each(*group(3), lambda j: draw_half(to(relay(j)), 0))
+    each(*group(2), lambda j: forward(j, 1))
+    each(*group(3), lambda j: draw_half(to(relay(j)), 1))
+    each(*group(2), share)
+    for p in range(2):
+        each(*group(2), lambda j: finish(j, p))
+    each(*group(2), use)
+    each(*group(3), lambda j: forward(j, 0))
+    each(*group(2), lambda j: use(relay(j)))
+    each(*group(3), lambda j: forward(j, 1))
+    each(*group(3), share)
+    each(*group(3), use)
+
+    def use_mine(j):
+        scale_copy(relay(j), to(relay(j))).wait_recv()
+        multiply_half(relay(j), g, mine)
+
+    each(*group(3), use_mine)
+    for p in range(2):
+        each(*group(3), lambda j: finish(j, p))
+    each(*group(3), lambda j: multiply_half(relay(j), 1 - g, theirs))
 
     mean_copy(1 - c).wait_recv()
 
@@ -307,12 +345,12 @@
         for k in mine:
             net(step, me, k).wait_send()
 
-    @pl.loop(1, quarter)
+    @pl.loop(1, near)
     def _(step):
         for k in theirs:
             net(step, me, k).wait_send()
 
-    @pl.loop(quarter, n)
+    @pl.loop(near, n)
     def _(step):
         for p, k in enumerate(mine):
             row_copy(step, to(step), k, p).wait_send()

time: 76.2 us -> 75.6 us (level)
  no operation moved by 1% of the time
where the time goes in v1:
time: 75.6 us; the launch traced here: 75.4 us
  Pallas kernels  71 us (94%)
  local copies, waits for them, and re-layouts  3.74 us (5%)
    pallas_call x1, Pallas kernels, on_device(): pl.pallas_call(functools.partial(kernel, n), out_shape=(jax.ShapeDtypeStr...  71 us
    unnamed x4, local copies, waits for them, and re-layouts  3.74 us

profile of v1, /device:TPU:0, one launch (start us, length us, event | category | flops | bytes accessed | tf_op | source)
XLA Modules:
  0.0 75.4 jit_solution(5402215543024686991)
XLA Ops:
  0.6 71.0 %shard_map.59 = (f32[256,2048]{1,0:T(8,128)}, f32[1,2048]{1,0:T(1,128)}) custom-call(f32[512,2048]{1,0:T(8,128)} %basis.1, f32[1,512]{1,0:T(1,128)} %bitcast.6, f32[1,256]{1,0:T(1,128)} %bitcast.7, s32[1,2048]{1,0:T(1,128)} %bitcast.4), custom_call_target="tpu_custom_call" | custom-call | tf_op jit(solution)/shard_map/pallas_call | solution.py:374
  71.6 0.0 copy-start
  71.7 3.1 %copy.8 = f32[256,2048]{1,0:T(8,128)} copy(f32[256,2048]{1,0:T(8,128)} %get-tuple-element.8) | data formatting | bytes 4194304
  74.8 0.0 copy-done
  74.8 0.6 copy.9
Async XLA Ops:
  71.6 3.2 %copy-start = (f32[1,2048]{1,0:T(1,128)S(1)}, f32[1,2048]{1,0:T(1,128)}, u32[]{:S(2)}) copy-start(f32[1,2048]{1,0:T(1,128)} %get-tuple-element.5) | copy-start | bytes 24580

commit v2 on v1

v2 whole, which is shorter than its diff:
```python
import functools
import math

import jax
import jax.numpy as jnp
import numpy as np
from jax import lax
from jax.experimental import pallas as pl
from jax.experimental.pallas import tpu as pltpu
from jax.sharding import PartitionSpec as P

MESH = pl.DeviceIdType.MESH
PIECES = 8


def sine_series():
    points = 0.25 * np.cos((np.arange(200) + 0.5) * np.pi / 400)
    powers = points[:, None] ** np.arange(0, 9, 2)[None, :]
    values = np.sin(2 * np.pi * points) / points
    return [float(c) for c in np.linalg.lstsq(powers, values, rcond=None)[0]]


SINE = sine_series()


def scramble(word):
    word = word ^ lax.shift_right_logical(word, jnp.int32(15))
    word = word * jnp.int32(-2048144789)
    word = word ^ lax.shift_right_logical(word, jnp.int32(13))
    word = word * jnp.int32(-1028477387)
    return word ^ lax.shift_right_logical(word, jnp.int32(16))


def normals(seed_terms, counter_terms):
    start_word = seed_terms + counter_terms
    first_word = scramble(start_word) & jnp.int32(16777215)
    second_word = scramble(start_word + jnp.int32(668265261)) & jnp.int32(16777215)
    first_unit = (first_word.astype(jnp.float32) + 0.5) * (1.0 / 16777216.0)
    square = -2.0 * jnp.log(first_unit)
    radius = square * lax.rsqrt(jnp.maximum(square, 1e-30))
    folded = jnp.abs(second_word.astype(jnp.float32) - 8388607.5) - 4194304.0
    turn = folded * (1.0 / 16777216.0)
    turn2 = turn * turn
    series = jnp.full_like(turn, SINE[-1])
    for coefficient in SINE[-2::-1]:
        series = series * turn2 + coefficient
    return (radius * turn) * series


def split(values):
    high = values.astype(jnp.bfloat16)
    return high, (values - high.astype(jnp.float32)).astype(jnp.bfloat16)


def kernel(n, basis, scales, mean, seeds, modulus, means, gathered, scale_all, mean_all, seed_row, coefs, lhs,
           total, staged, parts, near_recv, far_recv, extra_recv, net_send, row_recv, row_send, core_recv, core_send,
           scale_send, scale_recv, mean_sems, own_sem, part_recv, part_send, out_sems, small_sems):
    g, me, c = lax.axis_index("grp"), lax.axis_index("mode"), lax.axis_index("node")
    _, _, pieces, piece, wide = gathered.shape
    rows, deep = pieces * piece, pieces // 2
    half = rows // 2
    last = deep - 1
    samples = coefs.shape[-1]
    across, sibling = (1 - g, me, c), (g, me, 1 - c)
    mine, theirs = [[side * deep + p for p in range(deep)] for side in (g, 1 - g)]

    def to(step):
        flipped, bit = 0, 1
        while bit < n:
            flipped = flipped + lax.rem(me // bit + step // bit, 2) * bit
            bit *= 2
        return flipped

    near, quarter, eighth = n // 2, n // 4, n // 8
    inner = lax.rem(me // near + me // quarter, 2)

    def far(q):
        return near + quarter - 1 - q // 2 + lax.rem(q, 2) * quarter

    def relay(j):
        base = n - 1 - j
        return base + inner * (quarter * (1 - 2 * ((base // quarter) % 2)))

    def each(low, high, body):
        if high - low == 1:
            body(low)
        else:
            pl.loop(low, high)(body)

    def group(index):
        return index * eighth, (index + 1) * eighth

    def outside(*actions):
        @pl.when(inner == 0)
        def _():
            for action in actions:
                action()

    def inside(*actions):
        @pl.when(inner == 1)
        def _():
            for action in actions:
                action()

    def settle(block, sem):
        pltpu.make_async_copy(block, block, sem).wait()

    barrier = pltpu.get_barrier_semaphore()

    @pl.loop(1, n)
    def _(step):
        pl.semaphore_signal(barrier, inc=1, device_id=(g, to(step), c), device_id_type=MESH)
        pl.semaphore_signal(barrier, inc=1, device_id=(g, to(step), 1 - c), device_id_type=MESH)

    pl.semaphore_signal(barrier, inc=1, device_id=across, device_id_type=MESH)
    pl.semaphore_signal(barrier, inc=1, device_id=sibling, device_id_type=MESH)

    small = [
        pltpu.make_async_copy(scales, scale_all.at[me], small_sems.at[0]),
        pltpu.make_async_copy(mean, mean_all.at[c], small_sems.at[1]),
        pltpu.make_async_copy(seeds.at[:, pl.ds(pl.multiple_of(c * samples, 128), samples)], seed_row, small_sems.at[2]),
    ]
    for copy in small:
        copy.start()
    own_columns = pl.ds(pl.multiple_of(me * wide, 128), wide)
    for k in range(pieces):
        pltpu.make_async_copy(
            basis.at[pl.ds(k * piece, piece), own_columns], gathered.at[c, me, k], own_sem.at[0]).start()
    for copy in small:
        copy.wait()
    pl.semaphore_wait(barrier, 2 * n)

    def net(step, owner, k, send_sem, recv_sem):
        peer = to(step)
        return pltpu.make_async_remote_copy(
            src_ref=basis.at[pl.ds(pl.multiple_of(k * piece, 8), piece), pl.ds(pl.multiple_of(peer * wide, 128), wide)],
            dst_ref=gathered.at[c, owner, k],
            send_sem=send_sem, recv_sem=recv_sem, device_id=(g, peer, c), device_id_type=MESH)

    def far_copy(step, owner, p):
        return net(step, owner, mine[p], net_send.at[0], far_recv.at[p, step - near])

    def near_copy(step, owner, k):
        return net(step, owner, k, net_send.at[1], near_recv.at[k // deep, step])

    def extra_copy(j, owner):
        return net(relay(j), owner, theirs[last], net_send.at[2], extra_recv.at[j - 3 * eighth])

    def scale_copy(step, owner):
        return pltpu.make_async_remote_copy(
            src_ref=scale_all.at[me], dst_ref=scale_all.at[owner],
            send_sem=scale_send.at[0], recv_sem=scale_recv.at[step], device_id=(g, to(step), c), device_id_type=MESH)

    def row_copy(j, owner, p):
        block = gathered.at[c, owner, mine[p]]
        sem = row_send.at[(j - 3 * eighth + near) // near]
        return pltpu.make_async_remote_copy(
            src_ref=block, dst_ref=block,
            send_sem=sem, recv_sem=row_recv.at[2 * p // deep, relay(j) - near], device_id=across, device_id_type=MESH)

    def core_copy(step, owner, k, h, side):
        block = gathered.at[side, owner, k]
        return pltpu.make_async_remote_copy(
            src_ref=block, dst_ref=block,
            send_sem=core_send.at[0], recv_sem=core_recv.at[h, step],
            device_id=sibling, device_id_type=MESH)

    def part_copy(step, owner, source, target):
        return pltpu.make_async_remote_copy(
            src_ref=parts.at[c, me], dst_ref=parts.at[source, owner],
            send_sem=part_send.at[lax.rem(target + c, 2)], recv_sem=part_recv.at[lax.rem(source + target, 2)],
            device_id=(g, to(step), target), device_id_type=MESH)

    mean_copy = lambda side: pltpu.make_async_remote_copy(
        src_ref=mean_all.at[c], dst_ref=mean_all.at[side], send_sem=mean_sems.at[0], recv_sem=mean_sems.at[1],
        device_id=sibling, device_id_type=MESH)

    @pl.loop(1, n)
    def _(step):
        scale_copy(step, me).start()

    mean_copy(c).start()

    @pl.loop(0, near)
    def _(q):
        for p in range(deep):
            far_copy(far(q), me, p).start()

    inside(lambda: each(*group(3), lambda j: extra_copy(j, me).start()))

    @pl.loop(quarter, near)
    def _(step):
        for k in range(pieces):
            near_copy(step, me, k).start()

    @pl.loop(1, quarter)
    def _(step):
        for k in range(pieces):
            near_copy(step, me, k).start()

    settle(gathered.at[c, me], own_sem.at[0])
    for k in range(pieces):
        core_copy(0, me, k, k // deep, c).start()

    seed_terms = seed_row[...] * jnp.int32(-1640531527)
    lanes = min(512, samples)
    tiles = half // 16

    def draw_half(owner, side):
        @pl.loop(0, tiles)
        def _(tile):
            first = owner * rows + side * half + tile * 16
            ids = lax.broadcasted_iota(jnp.int32, (16, lanes), 0) + first
            counters = ids * jnp.int32(2 * 668265261 - 2**32 if 2 * 668265261 >= 2**31 else 2 * 668265261)
            for start in range(0, samples, lanes):
                high, low = split(normals(seed_terms[:, start:start + lanes], counters))
                for part, values in enumerate((high, low, high)):
                    here = pl.ds(pl.multiple_of((3 * side + part) * half + tile * 16, 16), 16)
                    coefs[owner, here, start:start + lanes] = values

    def draw(owner):
        draw_half(owner, 0)
        draw_half(owner, 1)

    def accumulate(owner, first_row, depth, first):
        columns = min(1024, samples)

        @pl.loop(0, samples // columns)
        def _(tile):
            here = pl.ds(pl.multiple_of(tile * columns, 128), columns)
            product = jnp.dot(lhs[:, 0:depth], coefs[owner, pl.ds(first_row, depth), here], preferred_element_type=jnp.float32)
            if first:
                total[:, here] = product
            else:
                total[:, here] += product

    def scaled(step):
        scale_copy(step, to(step)).wait_recv()
        return step

    def arrived(step, owner, h):
        settle(gathered.at[1 - c, owner, pl.ds(h * deep, deep)], core_recv.at[h, step])

    def multiply(step, first):
        owner = to(step)
        for h in range(2):
            arrived(step, owner, h)
        for side in range(2):
            block = gathered[side, owner].reshape(rows, wide)
            high, low = split(block.T * scale_all[owner])
            for h in range(2):
                for part, values in enumerate((high, high, low)):
                    at = (3 * h + part) * half
                    lhs[side * wide:(side + 1) * wide, at:at + half] = values[:, h * half:(h + 1) * half]
        accumulate(owner, 0, 3 * rows, first)

    def multiply_half(step, h):
        owner = to(step)
        arrived(step, owner, h)
        scale_row = jnp.where(h == 0, scale_all[owner][:, 0:half], scale_all[owner][:, half:rows])
        for side in range(2):
            block = gathered[side, owner, pl.ds(h * deep, deep)].reshape(half, wide)
            high, low = split(block.T * scale_row)
            for part, values in enumerate((high, high, low)):
                lhs[side * wide:(side + 1) * wide, part * half:(part + 1) * half] = values
        accumulate(owner, pl.multiple_of(h * (3 * half), 16), 3 * half, False)

    def forward(j, p, relayed=True):
        step = relay(j)
        owner = to(step)
        far_copy(step, owner, p).wait_recv()
        if relayed:
            row_copy(j, owner, p).start()
        core_copy(step, owner, mine[p], g, c).start()

    def finish(j, ps, relayed):
        step = relay(j)
        owner = to(step)
        settle(gathered.at[c, owner, pl.ds(theirs[ps[0]], relayed)], row_recv.at[2 * ps[0] // deep, step - near])
        if relayed < len(ps):
            extra_copy(j, owner).wait_recv()
        for p in ps:
            core_copy(step, owner, theirs[p], 1 - g, c).start()

    def forwards(index, *ps):
        for p in ps:
            each(*group(index), lambda j: forward(j, p))

    def forward_last(index):
        each(*group(index), lambda j: forward(j, last, False))

    def finishes(index, *halves, relayed=deep // 2):
        for ps in halves:
            each(*group(index), lambda j: finish(j, ps, relayed))

    def share(step, h):
        owner = to(step)
        settle(gathered.at[c, owner, pl.ds(h * deep, deep)], near_recv.at[h, step])
        for k in range(h * deep, (h + 1) * deep):
            core_copy(step, owner, k, h, c).start()

    def share_near(index, *hs):
        for h in hs:
            each(*group(index), lambda step: share(step, h))

    def draw_far(index, side):
        each(*group(index), lambda j: draw_half(to(relay(j)), side))

    def draw_near(index, side):
        each(*group(index), lambda step: draw_half(to(step), side))

    def use_far(index):
        each(*group(index), lambda j: multiply(scaled(relay(j)), False))

    def use_near(index, h):
        each(*group(index), lambda step: multiply_half(step if h else scaled(step), h))

    def use_mine(index):
        each(*group(index), lambda j: multiply_half(scaled(relay(j)), g))

    def use_theirs(index):
        each(*group(index), lambda j: multiply_half(relay(j), 1 - g))

    early, late = tuple(range(deep // 2)), tuple(range(deep // 2, deep))
    draw(me)
    each(1, quarter, lambda step: draw(to(step)))
    multiply(0, True)
    inside(lambda: forwards(0, *early, *late))
    draw_far(0, 0)
    outside(lambda: forwards(0, *early))
    draw_far(0, 1)
    draw_far(1, 0)
    outside(lambda: forwards(0, *late))
    inside(lambda: finishes(0, early))
    draw_far(1, 1)
    outside(lambda: finishes(0, early))
    inside(lambda: finishes(0, late), lambda: forwards(1, *early))
    draw_near(2, 0)
    inside(lambda: forwards(1, *late))
    for h in range(2):
        each(1, quarter, lambda step: share(step, h))
    draw_near(2, 1)
    outside(lambda: finishes(0, late), lambda: forwards(1, *early))
    each(1, quarter, lambda step: multiply(scaled(step), False))
    inside(lambda: finishes(1, early))
    use_far(0)
    outside(lambda: forwards(1, *late))
    inside(lambda: finishes(1, late))
    draw_far(2, 0)
    outside(lambda: forwards(2, 0))
    draw_far(2, 1)
    outside(lambda: forwards(2, 1, 2), lambda: finishes(1, early))
    draw_near(3, 0)
    outside(lambda: forwards(2, 3), lambda: finishes(1, late))
    draw_near(3, 1)
    inside(lambda: forwards(2, *early))
    use_far(1)
    inside(lambda: forwards(2, 2))
    draw_far(3, 0)
    inside(lambda: forwards(2, 3))
    share_near(2, 0, 1)
    draw_far(3, 1)
    outside(lambda: finishes(2, early, late), lambda: forwards(3, 0, 1, 2))
    use_near(2, 0)
    outside(lambda: forwards(3, 3))
    use_near(2, 1)
    use_mine(2)
    inside(lambda: forwards(3, 0), lambda: finishes(2, early, late))
    share_near(3, 0)
    inside(lambda: forwards(3, 1))
    use_near(3, 0)
    inside(lambda: forwards(3, 2))
    use_theirs(2)
    inside(lambda: forward_last(3))
    outside(lambda: finishes(3, early))
    inside(lambda: share_near(3, 1), lambda: finishes(3, early))
    use_mine(3)
    outside(lambda: finishes(3, late), lambda: share_near(3, 1))
    inside(lambda: finishes(3, late, relayed=deep // 2 - 1))
    use_near(3, 1)
    use_theirs(3)

    mean_copy(1 - c).wait_recv()

    sums = jnp.zeros((1, samples), jnp.float32)
    for side in range(2):
        shift = jnp.broadcast_to(mean_all[side], (8, wide)).T[:, :1]
        values = jnp.exp(total[side * wide:(side + 1) * wide, :] + shift)
        staged[side] = values
        sums = sums + jnp.sum(values, axis=0, keepdims=True)
    parts[c, me] = sums
    out_columns = modulus.at[:, pl.ds(pl.multiple_of(c * samples, 128), samples)]
    other_columns = modulus.at[:, pl.ds(pl.multiple_of((1 - c) * samples, 128), samples)]
    local_out = pltpu.make_async_copy(staged.at[c], out_columns, out_sems.at[0])
    send_out = lambda landing: pltpu.make_async_remote_copy(
        src_ref=staged.at[1 - c], dst_ref=landing, send_sem=out_sems.at[1], recv_sem=out_sems.at[2],
        device_id=sibling, device_id_type=MESH)

    @pl.loop(1, n)
    def _(step):
        part_copy(step, me, c, c).start()
        part_copy(step, me, c, 1 - c).start()

    part_copy(0, me, c, 1 - c).start()
    send_out(out_columns).start()
    local_out.start()

    mean_copy(c).wait_send()
    settle(scale_all.at[0:n - 1], scale_send.at[0])
    settle(gathered.at[0, 0:near, 0:deep], net_send.at[0])
    settle(gathered.at[0, 0:near - 1], net_send.at[1])
    settle(gathered.at[0], core_send.at[0])
    settle(gathered.at[0, 0:3 * eighth, 0:deep], row_send.at[0])
    outside(lambda: settle(gathered.at[0, 0:eighth, 0:deep], row_send.at[1]))
    inside(lambda: settle(gathered.at[0, 0:eighth, 0:last], row_send.at[1]),
           lambda: settle(gathered.at[0, 0:eighth, 0], net_send.at[2]))
    settle(parts.at[0, 0:n - 1], part_send.at[0])
    settle(parts.at[0], part_send.at[1])
    settle(parts.at[0, 0:n - 1], part_recv.at[0])
    settle(parts.at[0], part_recv.at[1])

    for side in range(2):
        summed = jnp.zeros((1, samples), jnp.float32)
        for m in range(n):
            summed = summed + parts[side, m]
        means[:, side * samples:(side + 1) * samples] = summed / (n * 2 * wide)
    local_out.wait()
    send_out(other_columns).wait_recv()
    send_out(out_columns).wait_send()


def on_device(mode_basis, mode_scales, mean_log, sample_seeds):
    n = lax.axis_size("mode")
    rows, wide, all_samples = mode_scales.shape[0], mean_log.shape[0], sample_seeds.shape[0]
    piece, samples, near = rows // PIECES, all_samples // 2, n // 2
    vmem = pl.BlockSpec(memory_space=pltpu.VMEM)
    anywhere = pl.BlockSpec(memory_space=pl.ANY)
    dma = pltpu.SemaphoreType.DMA
    modulus, means = pl.pallas_call(
        functools.partial(kernel, n),
        out_shape=(
            jax.ShapeDtypeStruct((wide, all_samples), jnp.float32),
            jax.ShapeDtypeStruct((1, all_samples), jnp.float32),
        ),
        in_specs=[anywhere] * 4,
        out_specs=(anywhere, vmem),
        scratch_shapes=[
            pltpu.VMEM((2, n, PIECES, piece, wide), jnp.float32),
            pltpu.VMEM((n, 1, rows), jnp.float32),
            pltpu.VMEM((2, 1, wide), jnp.float32),
            pltpu.VMEM((1, samples), jnp.int32),
            pltpu.VMEM((n, 3 * rows, samples), jnp.bfloat16),
            pltpu.VMEM((2 * wide, 3 * rows), jnp.bfloat16),
            pltpu.VMEM((2 * wide, samples), jnp.float32),
            pltpu.VMEM((2, wide, samples), jnp.float32),
            pltpu.VMEM((2, n, 1, samples), jnp.float32),
            dma((2, near)), dma((PIECES // 2, near)), dma((n // 8,)), dma((3,)), dma((2, near)), dma((2,)), dma((2, n)), dma((1,)),
            dma((1,)), dma((n,)), dma((2,)), dma((1,)), dma((2,)), dma((2,)), dma((3,)), dma((3,)),
        ],
        compiler_params=pltpu.CompilerParams(
            collective_id=0, has_side_effects=True, vmem_limit_bytes=60 * 1024 * 1024
        ),
    )(mode_basis, mode_scales[None, :], mean_log[None, :], sample_seeds[None, :])
    return modulus, means[0]


def solution(mesh):
    return jax.shard_map(
        on_device,
        mesh=mesh,
        in_specs=(P("mode", "node"), P("mode"), P(("node", "mode")), P("grp")),
        out_specs=(P(("node", "mode"), "grp"), P("grp")),
        check_vma=False,
    )
```

time: 75.6 us -> 68.7 us (0.909)
  Pallas kernels: 71 us -> 64.1 us
    pallas_call x1, Pallas kernels: 71 us -> 64.1 us  [on_device(): pl.pallas_call(functools.partial(kernel, n), out_shape=(jax.ShapeDtypeStr...]
where the time goes in v2:
time: 68.7 us; the launch traced here: 68.5 us
  Pallas kernels  64.1 us (93%)
  local copies, waits for them, and re-layouts  3.74 us (5%)
    pallas_call x1, Pallas kernels, on_device(): pl.pallas_call(functools.partial(kernel, n), out_shape=(jax.ShapeDtypeStr...  64.1 us
    unnamed x4, local copies, waits for them, and re-layouts  3.74 us

profile of v2, /device:TPU:0, one launch (start us, length us, event | category | flops | bytes accessed | tf_op | source)
XLA Modules:
  0.0 68.5 jit_solution(5385936519824736068)
XLA Ops:
  0.6 64.1 %shard_map.59 = (f32[256,2048]{1,0:T(8,128)}, f32[1,2048]{1,0:T(1,128)}) custom-call(f32[512,2048]{1,0:T(8,128)} %basis.1, f32[1,512]{1,0:T(1,128)} %bitcast.6, f32[1,256]{1,0:T(1,128)} %bitcast.7, s32[1,2048]{1,0:T(1,128)} %bitcast.4), custom_call_target="tpu_custom_call" | custom-call | tf_op jit(solution)/shard_map/pallas_call | solution.py:439
  64.7 0.0 copy-start
  64.7 3.1 %copy.8 = f32[256,2048]{1,0:T(8,128)} copy(f32[256,2048]{1,0:T(8,128)} %get-tuple-element.8) | data formatting | bytes 4194304
  67.9 0.0 copy-done
  67.9 0.6 copy.9
Async XLA Ops:
  64.7 3.2 %copy-start = (f32[1,2048]{1,0:T(1,128)S(1)}, f32[1,2048]{1,0:T(1,128)}, u32[]{:S(2)}) copy-start(f32[1,2048]{1,0:T(1,128)} %get-tuple-element.5) | copy-start | bytes 24580

commit v3 on v2

--- a/solution.py
+++ b/solution.py
@@ -230,9 +230,21 @@
             here = pl.ds(pl.multiple_of(tile * columns, 128), columns)
             product = jnp.dot(lhs[:, 0:depth], coefs[owner, pl.ds(first_row, depth), here], preferred_element_type=jnp.float32)
             if first:
-                total[:, here] = product
+                for spot, side in enumerate((1 - c, c)):
+                    shift = jnp.broadcast_to(mean_all[side], (8, wide)).T[:, :1]
+                    total[spot * wide:(spot + 1) * wide, here] = product[spot * wide:(spot + 1) * wide] + shift
             else:
                 total[:, here] += product
+
+    def conclude(owner, first_row, depth):
+        columns = min(256, samples)
+        for start in range(0, samples, columns):
+            here = slice(start, start + columns)
+            product = jnp.dot(lhs[:, 0:depth], coefs[owner, pl.ds(first_row, depth), here], preferred_element_type=jnp.float32)
+            values = jnp.exp(total[:, here] + product)
+            staged[:, here] = values[0:wide]
+            modulus[c, :, here] = values[wide:2 * wide]
+            parts[c, me, :, here] = jnp.sum(values, axis=0, keepdims=True)
 
     def scaled(step):
         scale_copy(step, to(step)).wait_recv()
@@ -245,25 +257,29 @@
         owner = to(step)
         for h in range(2):
             arrived(step, owner, h)
-        for side in range(2):
+        for spot, side in enumerate((1 - c, c)):
             block = gathered[side, owner].reshape(rows, wide)
             high, low = split(block.T * scale_all[owner])
             for h in range(2):
                 for part, values in enumerate((high, high, low)):
                     at = (3 * h + part) * half
-                    lhs[side * wide:(side + 1) * wide, at:at + half] = values[:, h * half:(h + 1) * half]
+                    lhs[spot * wide:(spot + 1) * wide, at:at + half] = values[:, h * half:(h + 1) * half]
         accumulate(owner, 0, 3 * rows, first)
 
-    def multiply_half(step, h):
+    def multiply_half(step, h, final=False):
         owner = to(step)
         arrived(step, owner, h)
         scale_row = jnp.where(h == 0, scale_all[owner][:, 0:half], scale_all[owner][:, half:rows])
-        for side in range(2):
+        for spot, side in enumerate((1 - c, c)):
             block = gathered[side, owner, pl.ds(h * deep, deep)].reshape(half, wide)
             high, low = split(block.T * scale_row)
             for part, values in enumerate((high, high, low)):
-                lhs[side * wide:(side + 1) * wide, part * half:(part + 1) * half] = values
-        accumulate(owner, pl.multiple_of(h * (3 * half), 16), 3 * half, False)
+                lhs[spot * wide:(spot + 1) * wide, part * half:(part + 1) * half] = values
+        first_row = pl.multiple_of(h * (3 * half), 16)
+        if final:
+            conclude(owner, first_row, 3 * half)
+        else:
+            accumulate(owner, first_row, 3 * half, False)
 
     def forward(j, p, relayed=True):
         step = relay(j)
@@ -324,6 +340,7 @@
     early, late = tuple(range(deep // 2)), tuple(range(deep // 2, deep))
     draw(me)
     each(1, quarter, lambda step: draw(to(step)))
+    mean_copy(1 - c).wait_recv()
     multiply(0, True)
     inside(lambda: forwards(0, *early, *late))
     draw_far(0, 0)
@@ -377,23 +394,22 @@
     use_mine(3)
     outside(lambda: finishes(3, late), lambda: share_near(3, 1))
     inside(lambda: finishes(3, late, relayed=deep // 2 - 1))
-    use_near(3, 1)
-    use_theirs(3)
-
-    mean_copy(1 - c).wait_recv()
-
-    sums = jnp.zeros((1, samples), jnp.float32)
-    for side in range(2):
-        shift = jnp.broadcast_to(mean_all[side], (8, wide)).T[:, :1]
-        values = jnp.exp(total[side * wide:(side + 1) * wide, :] + shift)
-        staged[side] = values
-        sums = sums + jnp.sum(values, axis=0, keepdims=True)
-    parts[c, me] = sums
-    out_columns = modulus.at[:, pl.ds(pl.multiple_of(c * samples, 128), samples)]
-    other_columns = modulus.at[:, pl.ds(pl.multiple_of((1 - c) * samples, 128), samples)]
-    local_out = pltpu.make_async_copy(staged.at[c], out_columns, out_sems.at[0])
-    send_out = lambda landing: pltpu.make_async_remote_copy(
-        src_ref=staged.at[1 - c], dst_ref=landing, send_sem=out_sems.at[1], recv_sem=out_sems.at[2],
+
+    def use_last(turn, low, high, final=False):
+        def body(step):
+            picked = lax.rem(inner + turn, 2)
+            multiply_half(picked * step + (1 - picked) * relay(step), picked + (1 - picked) * (1 - g), final)
+
+        if high > low:
+            each(low, high, body)
+
+    end = 4 * eighth
+    use_last(0, 3 * eighth, end)
+    use_last(1, 3 * eighth, end - 1)
+    use_last(1, end - 1, end, True)
+
+    send_out = lambda half_index: pltpu.make_async_remote_copy(
+        src_ref=staged, dst_ref=modulus.at[half_index], send_sem=out_sems.at[0], recv_sem=out_sems.at[1],
         device_id=sibling, device_id_type=MESH)
 
     @pl.loop(1, n)
@@ -402,8 +418,7 @@
         part_copy(step, me, c, 1 - c).start()
 
     part_copy(0, me, c, 1 - c).start()
-    send_out(out_columns).start()
-    local_out.start()
+    send_out(c).start()
 
     mean_copy(c).wait_send()
     settle(scale_all.at[0:n - 1], scale_send.at[0])
@@ -424,9 +439,23 @@
         for m in range(n):
             summed = summed + parts[side, m]
         means[:, side * samples:(side + 1) * samples] = summed / (n * 2 * wide)
-    local_out.wait()
-    send_out(other_columns).wait_recv()
-    send_out(out_columns).wait_send()
+    send_out(1 - c).wait_recv()
+    send_out(c).wait_send()
+
+
+def write_out(values, sums, modulus, means, sems):
+    rows, samples = values.shape[1:]
+    part = rows // 2
+    copies = [pltpu.make_async_copy(sums, means, sems.at[4])]
+    for side in range(2):
+        for block in range(2):
+            here = pl.ds(block * part, part)
+            copies.append(pltpu.make_async_copy(
+                values.at[side, here], modulus.at[here, side * samples:(side + 1) * samples], sems.at[2 * side + block]))
+    for copy in copies:
+        copy.start()
+    for copy in copies:
+        copy.wait()
 
 
 def on_device(mode_basis, mode_scales, mean_log, sample_seeds):
@@ -439,11 +468,11 @@
     modulus, means = pl.pallas_call(
         functools.partial(kernel, n),
         out_shape=(
-            jax.ShapeDtypeStruct((wide, all_samples), jnp.float32),
-            jax.ShapeDtypeStruct((1, all_samples), jnp.float32),
+            pltpu.VMEM((2, wide, samples), jnp.float32),
+            pltpu.VMEM((1, all_samples), jnp.float32),
         ),
         in_specs=[anywhere] * 4,
-        out_specs=(anywhere, vmem),
+        out_specs=(vmem, vmem),
         scratch_shapes=[
             pltpu.VMEM((2, n, PIECES, piece, wide), jnp.float32),
             pltpu.VMEM((n, 1, rows), jnp.float32),
@@ -452,21 +481,35 @@
             pltpu.VMEM((n, 3 * rows, samples), jnp.bfloat16),
             pltpu.VMEM((2 * wide, 3 * rows), jnp.bfloat16),
             pltpu.VMEM((2 * wide, samples), jnp.float32),
-            pltpu.VMEM((2, wide, samples), jnp.float32),
+            pltpu.VMEM((wide, samples), jnp.float32),
             pltpu.VMEM((2, n, 1, samples), jnp.float32),
             dma((2, near)), dma((PIECES // 2, near)), dma((n // 8,)), dma((3,)), dma((2, near)), dma((2,)), dma((2, n)), dma((1,)),
-            dma((1,)), dma((n,)), dma((2,)), dma((1,)), dma((2,)), dma((2,)), dma((3,)), dma((3,)),
+            dma((1,)), dma((n,)), dma((2,)), dma((1,)), dma((2,)), dma((2,)), dma((2,)), dma((3,)),
         ],
         compiler_params=pltpu.CompilerParams(
-            collective_id=0, has_side_effects=True, vmem_limit_bytes=60 * 1024 * 1024
+            collective_id=0, has_side_effects=True, vmem_limit_bytes=52 * 1024 * 1024
         ),
     )(mode_basis, mode_scales[None, :], mean_log[None, :], sample_seeds[None, :])
-    return modulus, means[0]
+    return pl.pallas_call(
+        write_out,
+        out_shape=(
+            jax.ShapeDtypeStruct((wide, all_samples), jnp.float32),
+            jax.ShapeDtypeStruct((1, all_samples), jnp.float32),
+        ),
+        in_specs=[vmem, vmem],
+        out_specs=(anywhere, anywhere),
+        scratch_shapes=[dma((5,))],
+        compiler_params=pltpu.CompilerParams(vmem_limit_bytes=1024 * 1024),
+    )(*(pltpu.with_memory_space_constraint(array, pltpu.VMEM) for array in (modulus, means)))
 
 
 def solution(mesh):
+    def call(*arrays):
+        modulus, means = on_device(*arrays)
+        return modulus, means[0]
+
     return jax.shard_map(
-        on_device,
+        call,
         mesh=mesh,
         in_specs=(P("mode", "node"), P("mode"), P(("node", "mode")), P("grp")),
         out_specs=(P(("node", "mode"), "grp"), P("grp")),

time: 68.7 us -> 65 us (0.946)
  local copies, waits for them, and re-layouts: 3.74 us -> 0 us
    unnamed x4 -> x0, local copies, waits for them, and re-layouts: 3.74 us -> none
    pallas_call x1 -> x2, Pallas kernels: 64.1 us -> 64 us  [the longest x1 62.7 us: on_device(): pl.pallas_call(functools.partial(kernel, n), out_shape=(pltpu.VMEM((2, wi...]
where the time goes in v3:
time: 65 us; the launch traced here: 64.8 us
  Pallas kernels  64 us (98%)
  between operations  0.8 us (1%)
    pallas_call x1, Pallas kernels, on_device(): pl.pallas_call(functools.partial(kernel, n), out_shape=(pltpu.VMEM((2, wi...  62.7 us
    pallas_call x1, Pallas kernels, on_device(): pl.pallas_call(write_out, out_shape=(jax.ShapeDtypeStruct((wide, all_samp...  1.36 us

profile of v3, /device:TPU:0, one launch (start us, length us, event | category | flops | bytes accessed | tf_op | source)
XLA Modules:
  0.0 64.8 jit_solution(3639262755509024147)
XLA Ops:
  0.6 62.7 %shard_map.59 = (f32[2,256,1024]{2,1,0:T(8,128)S(1)}, f32[1,2048]{1,0:T(1,128)S(1)}) custom-call(f32[512,2048]{1,0:T(8,128)} %basis.1, f32[1,512]{1,0:T(1,128)} %bitcast.5, f32[1,256]{1,0:T(1,128)} %bitcast.6, s32[1,2048]{1,0:T(1,128)} %bitcast.4), custom_call_target="tpu_custom_call" | custom-call | tf_op jit(solution)/shard_map/pallas_call | solution.py:468
  63.3 1.4 %shard_map.60 = (f32[256,2048]{1,0:T(8,128)}, f32[1,2048]{1,0:T(1,128)}) custom-call(f32[2,256,1024]{2,1,0:T(8,128)S(1)} %get-tuple-element.6.values, f32[1,2048]{1,0:T(1,128)S(1)} %get-tuple-element.7.sums), custom_call_target="tpu_custom_call" | custom-call | tf_op jit(solution)/shard_map/pallas_call | solution.py:493
